TPU v7x, 32 devices: a whole 2x2x4 slice. The times are simulated.
32 devices in a mesh: gx: 4 (over z), gy: 2 (over y), gz: 4 (over x, core).
Axes of the slice: x: 2, y: 2, z: 4, core: 2. Of those that a mesh axis runs over, the one named last changes fastest.
Arguments:
- strain: float32 [2, 4, 64, 32, 512], P(None, None, 'gx', 'gy', 'gz'), may hold values from -6 to 6
- cell_shell_index: int32 [64, 32, 512], P('gx', 'gy', 'gz'), may hold values from 0 to 255
- onset_step: int32 [256], replicated, may hold values from 0 to 1
Outputs:
- psi_four: float32 [2, 4, 64, 32, 512], P(None, None, 'gx', 'gy', 'gz')
- energy: float32 [4, 4, 256], P('gx', None, ('gy', 'gz'))
All inputs are finite; a program needn't handle non-finite values.
Results may differ from a plain program's by a relative error of at most 0.00007.
Values sent between devices are 32-bit elements; how exact they have to be, the bound alone decides.
A program may use at most 64 MiB of HBM per device.

v0:
```python
import jax
import jax.numpy as jnp
from jax import lax
from jax.sharding import PartitionSpec as P

first_coef = ((-2, 1.0), (-1, -8.0), (1, 8.0), (2, -1.0))
second_coef = ((-2, -1.0), (-1, 16.0), (0, -30.0), (1, 16.0), (2, -1.0))


def extended(cells, sides, width):
    for axis, dim in sides:
        count = lax.axis_size(axis)
        ends = count - 1
        head = lax.slice_in_dim(cells, 0, width, axis=dim)
        tail = lax.slice_in_dim(cells, cells.shape[dim] - width, cells.shape[dim], axis=dim)
        cells = jnp.concatenate(
            [
                lax.ppermute(tail, axis, [(i, (i + 1) % count) for i in range(ends)]),
                cells,
                lax.ppermute(head, axis, [((i + 1) % count, i) for i in range(ends)]),
            ],
            axis=dim,
        )
    return cells


def entering(value, axis, combine, identity):
    peers, here = (lax.axis_size(axis), lax.axis_index(axis))
    everything = lax.all_gather(value, axis)
    start = jnp.broadcast_to(jnp.asarray(identity, value.dtype), value.shape)

    def turn(k, before):
        reached = k < here
        new = combine(before, everything[k])
        return jnp.where(reached, new, before)

    return lax.fori_loop(0, peers, turn, start)


def along_z(padded, cells_z):
    views = {}
    for offset in (-2, -1, 0, 1, 2):
        views[offset] = padded[:, :, :, :, 2 + offset : 2 + offset + cells_z]
    first_z = sum((w * views[k] for k, w in first_coef)) / 12.0
    second_z = sum((w * views[k] for k, w in second_coef)) / 12.0
    return (views[0], first_z, second_z)


def body(strain, cell_shell_index, onset_step):
    cells_x, cells_y, cells_z = (strain.shape[2], strain.shape[3], strain.shape[4])
    steps_count = strain.shape[1]
    shell_count = onset_step.shape[0]
    padded = extended(strain, (("gx", 2), ("gy", 3), ("gz", 4)), 2)
    center, first_z, second_zfull = along_z(padded, cells_z)
    mixed_yz = (
        sum((w * first_z[:, :, 2 : 2 + cells_x, 2 + k : 2 + k + cells_y, :] for k, w in first_coef))
        / 12.0
    )
    second_x = (
        sum((w * center[:, :, 2 + k : 2 + k + cells_x, 2 : 2 + cells_y, :] for k, w in second_coef))
        / 12.0
    )
    second_y = (
        sum((w * center[:, :, 2 : 2 + cells_x, 2 + k : 2 + k + cells_y, :] for k, w in second_coef))
        / 12.0
    )
    second_z = second_zfull[:, :, 2 : 2 + cells_x, 2 : 2 + cells_y, :]
    combo = second_x + second_y - second_z
    real_part = 0.5 * combo[0] - mixed_yz[1]
    imag_part = -0.5 * combo[1] - mixed_yz[0]
    psi_four = jnp.stack([real_part, imag_part])
    bondi_news = jnp.cumsum(psi_four, axis=1) * 0.25
    total_x = cells_x * lax.axis_size("gx")
    total_y = cells_y * lax.axis_size("gy")
    total_z = cells_z * lax.axis_size("gz")
    start_x = (lax.axis_index("gx") * cells_x).astype(jnp.float32)
    start_y = (lax.axis_index("gy") * cells_y).astype(jnp.float32)
    start_z = (lax.axis_index("gz") * cells_z).astype(jnp.float32)
    position_along_x = (jnp.arange(cells_x, dtype=jnp.float32) + start_x + 0.5) / total_x - 0.5
    position_along_y = (jnp.arange(cells_y, dtype=jnp.float32) + start_y + 0.5) / total_y - 0.5
    position_along_z = (jnp.arange(cells_z, dtype=jnp.float32) + start_z + 0.5) / total_z - 0.5
    radius_squared = (
        position_along_x[:, None, None] ** 2
        + position_along_y[None, :, None] ** 2
        + position_along_z[None, None, :] ** 2
        + 0.05
    )
    energy_flux = radius_squared[None] * (bondi_news[0] ** 2 + bondi_news[1] ** 2)
    plane_len = cells_y * cells_z
    flux_planes = energy_flux.reshape(steps_count, cells_x, plane_len)
    shell_planes = cell_shell_index.reshape(cells_x, plane_len)
    shell_labels = jnp.arange(shell_count, dtype=jnp.int32)

    def bin_plane(total, pieces):
        shell_piece, plane = pieces
        flux_piece = lax.dynamic_index_in_dim(flux_planes, plane, 1, keepdims=False)
        one_hot = (shell_piece[:, None] == shell_labels[None, :]).astype(jnp.float32)
        return (total + jnp.dot(flux_piece, one_hot, precision=lax.Precision.HIGHEST), None)

    binned, unused = lax.scan(
        bin_plane,
        jnp.zeros((steps_count, shell_count), jnp.float32),
        (shell_planes, jnp.arange(cells_x, dtype=jnp.int32)),
    )
    live = (jnp.arange(steps_count, dtype=jnp.int32)[:, None] >= onset_step[None, :]).astype(
        jnp.float32
    )
    scale = 0.25 * shell_count / (total_x * total_y * total_z)
    partial_value = jnp.cumsum(binned * live, axis=0) * scale

    def add_terms(earlier, later):
        return earlier + later

    before = entering(partial_value, "gx", add_terms, jnp.zeros_like(partial_value))
    inclusive = before + partial_value
    energy = lax.psum_scatter(inclusive, ("gy", "gz"), scatter_dimension=1, tiled=True)[None]
    return (psi_four, energy)


def solution(mesh):
    placed = (P(None, None, "gx", "gy", "gz"), P("gx", "gy", "gz"), P())
    return jax.shard_map(
        body,
        mesh=mesh,
        in_specs=placed,
        out_specs=(P(None, None, "gx", "gy", "gz"), P("gx", None, ("gy", "gz"))),
        check_vma=False,
    )
```

profile of v0, /device:TPU:0, one launch (start us, length us, event | category | flops | bytes accessed | tf_op | source)
XLA Modules:
  0.0 202.8 jit_solution(14584290228002413221)
XLA Ops:
  7.2 1.6 constant_dynamic-update-slice_fusion.1
  8.9 5.0 %collective-permute-start = (f32[2,4,2,16,128]{4,2,3,1,0:T(2,128)S(1)}, f32[2,4,2,16,128]{4,2,3,1,0:T(2,128)S(1)}, u32[]{:S(2)}, u32[]{:S(2)}) collective-permute-start(f32[2,4,2,16,128]{4,2,3,1,0:T(2,128)S(1)} %get-tuple-element.189), channel_id=1, source_target_pairs={{0,8},{8,16},{16,24},{1,9},{9,17},{17,25},{2,10},{10,18},{18,26},{... | collective-permute-start | bytes 393224 | tf_op jit(solution)/shard_map/ppermute | solution.py:18
  13.9 1.3 collective-permute-start.1
  15.3 1.3 collective-permute-done
  16.6 4.1 %collective-permute-done.1 = f32[2,4,2,16,128]{4,2,3,1,0:T(2,128)S(1)} collective-permute-done((f32[2,4,2,16,128]{4,2,3,1,0:T(2,128)S(1)}, f32[2,4,2,16,128]{4,2,3,1,0:T(2,128)S(1)}, u32[]{:S(2)}, u32[]{:S(2)}) %collective-permute-start.1) | collective-permute-done | bytes 131104 | tf_op jit(solution)/shard_map/ppermute | solution.py:20
  21.5 3.4 %collective-permute-start.2 = (f32[2,4,20,2,128]{4,2,3,1,0:T(8,128)}, f32[2,4,20,2,128]{4,2,3,1,0:T(8,128)S(1)}, u32[]{:S(2)}, u32[]{:S(2)}) collective-permute-start(f32[2,4,20,2,128]{4,2,3,1,0:T(8,128)} %get-tuple-element.185), channel_id=1, source_target_pairs={{0,4},{1,5},{2,6},{3,7},{8,12},{9,13},{10,14},{11,15},{16,20},{17,... | collective-permute-start | bytes 491528 | tf_op jit(solution)/shard_map/ppermute | solution.py:18
  24.9 1.3 collective-permute-start.3
  27.0 1.6 copy.41
  28.7 1.1 copy-done.2
  29.8 2.8 %collective-permute-done.3 = f32[2,4,20,2,128]{4,2,3,1,0:T(8,128)} collective-permute-done((f32[2,4,20,2,128]{4,2,3,1,0:T(8,128)S(1)}, f32[2,4,20,2,128]{4,2,3,1,0:T(8,128)}, u32[]{:S(2)}, u32[]{:S(2)}) %collective-permute-start.3) | collective-permute-done | bytes 163872 | tf_op jit(solution)/shard_map/ppermute | solution.py:20
  32.6 1.2 pad_maximum_fusion.1
  33.8 2.5 %fusion.33 = (f32[2,4,20,20,2]{4,2,3,1,0:T(8,128)}, f32[2,4,20,20,2]{4,2,3,1,0:T(8,128)}) fusion(f32[2,4,20,20,128]{4,2,3,1,0:T(8,128)S(1)} %pad_maximum_fusion.1), kind=kLoop, calls=%fused_computation.84 | loop fusion | bytes 102400 | tf_op jit(solution)/shard_map/slice | solution.py:15
  36.3 3.4 %copy.22 = f32[2,4,20,20,2]{3,2,4,1,0:T(8,128)} copy(f32[2,4,20,20,2]{4,2,3,1,0:T(8,128)} %get-tuple-element.179) | data formatting | bytes 51200 | tf_op jit(solution)/shard_map/slice | solution.py:15
  39.7 2.0 collective-permute-start.4
  41.7 3.4 %copy.24 = f32[2,4,20,20,2]{3,2,4,1,0:T(8,128)} copy(f32[2,4,20,20,2]{4,2,3,1,0:T(8,128)} %get-tuple-element.180) | data formatting | bytes 51200 | tf_op jit(solution)/shard_map/slice | solution.py:14
  45.1 1.3 collective-permute-start.5
  46.4 3.1 %maximum_maximum_fusion.1 = (f32[2,4,20,18,128]{4,2,3,1,0:T(8,128)}, f32[2,4,20,18,128]{4,2,3,1,0:T(8,128)}) fusion(f32[2,4,2,16,128]{4,2,3,1,0:T(2,128)S(1)} %collective-permute-done.1, f32[2,4,16,16,128]{4,2,3,1,0:T(8,128)S(1)} %get-tuple-element.188, f32[2,4,2,16,128]{4,2,3,1,0:T(2,128)S(1)} %collective-permute-done, ...), kind=kLoop, calls=%fused_computation.15 | loop fusion | flops 2211840 | bytes 4587520 | tf_op jit(solution)/shard_map/concatenate | solution.py:16
  49.5 3.5 %copy.23 = f32[2,4,20,20,2]{4,2,3,1,0:T(8,128)} copy(f32[2,4,20,20,2]{3,2,4,1,0:T(8,128)} %collective-permute-done.4) | data formatting | bytes 51200 | tf_op jit(solution)/shard_map/ppermute | solution.py:18
  53.0 3.5 %copy.25 = f32[2,4,20,20,2]{4,2,3,1,0:T(8,128)} copy(f32[2,4,20,20,2]{3,2,4,1,0:T(8,128)} %collective-permute-done.5) | data formatting | bytes 51200 | tf_op jit(solution)/shard_map/ppermute | solution.py:20
  56.4 5.8 %maximum_maximum_fusion = (f32[2,4,20,20,130]{4,2,3,1,0:T(8,128)S(1)}, f32[2,4,20,20,130]{4,2,3,1,0:T(8,128)}) fusion(f32[2,4,20,2,128]{4,2,3,1,0:T(8,128)} %collective-permute-done.3, f32[2,4,2,16,128]{4,2,3,1,0:T(2,128)S(1)} %collective-permute-done.1, f32[2,4,16,16,128]{4,2,3,1,0:T(8,128)S(1)} %get-tuple-element.188, ...), kind=kLoop, calls=%fused_computation.10 | loop fusion | flops 4160000 | bytes 5017600 | tf_op jit(solution)/shard_map/concatenate | solution.py:16
  62.2 8.1 %fusion.32 = (f32[2,4,20,20,128]{4,2,3,1,0:T(8,128)}, f32[2,4,20,20,128]{4,2,3,1,0:T(8,128)S(1)}, f32[2,4,20,20,128]{4,2,3,1,0:T(8,128)}, f32[2,4,20,20,128]{4,2,3,1,0:T(8,128)}, f32[2,4,20,20,128]{4,2,3,1,0:T(8,128)}) fusion(f32[2,4,20,20,130]{4,2,3,1,0:T(8,128)S(1)} %get-tuple-element.181, f32[2,4,20,20,130]{4,2,3,1,0:T(8,128)} %get-tuple-element.182), kind=kLoop, calls=%fused_computation.83 | loop fusion | flops 2867200 | bytes 14745600 | tf_op jit(solution)/shard_map/slice | solution.py:43
  70.7 1.0 copy-done
  72.8 4.1 %fusion.15 = f32[2,4,16,16,128]{4,2,3,1,0:T(8,128)S(1)} fusion(f32[2,4,2,16,128]{4,2,3,1,0:T(2,128)S(1)} %collective-permute-done, f32[2,4,16,16,128]{4,2,3,1,0:T(8,128)S(1)} %get-tuple-element.188, f32[2,4,20,20,128]{4,2,3,1,0:T(8,128)} %get-tuple-element.175, f32[2,4,20,20,128]{4,2,3,1,0:T(8,128)} %get-tuple-element.174, ...), kind=kLoop, calls=%fused_computation.28 | loop fusion | flops 8126464 | bytes 13762560 | tf_op jit(solution)/shard_map/sub | solution.py:68
  78.4 67.7 %while.25 = (s32[]{:T(128)}, f32[4,256]{1,0:T(4,128)S(1)}, s32[16]{0:T(128)S(1)}, f32[4,16,2048]{2,1,0:T(8,128)S(1)}, s32[16,2048]{1,0:T(8,128)}, /*index=5*/s32[]{:T(128)}, s32[]{:T(128)}, s32[]{:T(128)}) while((s32[]{:T(128)}, f32[4,256]{1,0:T(4,128)S(1)}, s32[16]{0:T(128)S(1)}, f32[4,16,2048]{2,1,0:T(8,128)S(1)}, ...), condition=%wide.region_2.3_spmd.clone, body=%wide.region_1.2_spmd.clone.sunk | while | flops 25692164 | bytes 131221 | solution.py:100
  81.0 0.9 constant_dynamic-slice_fusion.4
  81.9 0.8 fusion.38
  85.2 0.9 constant_dynamic-slice_fusion.4
  86.1 0.8 fusion.38
  89.5 0.9 constant_dynamic-slice_fusion.4
  90.3 0.8 fusion.38
  93.7 0.9 constant_dynamic-slice_fusion.4
  94.5 0.8 fusion.38
  97.9 0.9 constant_dynamic-slice_fusion.4
  102.1 0.9 constant_dynamic-slice_fusion.4
  106.4 0.9 constant_dynamic-slice_fusion.4
  110.6 0.9 constant_dynamic-slice_fusion.4
  114.8 0.9 constant_dynamic-slice_fusion.4
  119.1 0.9 constant_dynamic-slice_fusion.4
  123.3 0.9 constant_dynamic-slice_fusion.4
  127.5 0.9 constant_dynamic-slice_fusion.4
  131.7 0.9 constant_dynamic-slice_fusion.4
  136.0 0.9 constant_dynamic-slice_fusion.4
  140.2 0.9 constant_dynamic-slice_fusion.4
  144.4 0.9 constant_dynamic-slice_fusion.4
  146.2 13.4 %all-gather.1 = f32[4,4,256]{2,1,0:T(4,128)S(1)} all-gather(f32[1,4,256]{2,1,0:T(4,128)S(1)} %multiply_bitcast_fusion), channel_id=2, replica_groups=mesh['gx'=4,'gy'=2,'gz'=4] {'gx'}, dimensions={0}, use_global_device_ids=true | all-gather | bytes 20480 | tf_op jit(solution)/shard_map/all_gather | solution.py:29
  160.7 1.3 copy.27
  162.0 32.7 %reduce-scatter.4.cloned.1.call-done = f32[32,4]{1,0:T(8,128)} async-done(((f32[256,4]{1,0:T(8,128)}), f32[32,4]{1,0:T(8,128)}) %reduce-scatter.4.cloned.1.call-update) | async-done | bytes 528
  194.6 1.4 copy.29
  (89 shorter events, 25.5 us)
Async XLA Ops:
  7.2 187.4 %reduce-scatter.4.cloned.1.call-start = ((), (), s32[]{:S(2)}) async-start(), calls=%async_computation.1 | async-start | bytes 147456
  8.9 7.7 %collective-permute-start = (f32[2,4,2,16,128]{4,2,3,1,0:T(2,128)S(1)}, f32[2,4,2,16,128]{4,2,3,1,0:T(2,128)S(1)}, u32[]{:S(2)}, u32[]{:S(2)}) collective-permute-start(f32[2,4,2,16,128]{4,2,3,1,0:T(2,128)S(1)} %get-tuple-element.189), channel_id=1, source_target_pairs={{0,8},{8,16},{16,24},{1,9},{9,17},{17,25},{2,10},{10,18},{18,26},{... | collective-permute-start | bytes 393224 | tf_op jit(solution)/shard_map/ppermute | solution.py:18
  13.9 6.9 %collective-permute-start.1 = (f32[2,4,2,16,128]{4,2,3,1,0:T(2,128)S(1)}, f32[2,4,2,16,128]{4,2,3,1,0:T(2,128)S(1)}, u32[]{:S(2)}, u32[]{:S(2)}) collective-permute-start(f32[2,4,2,16,128]{4,2,3,1,0:T(2,128)S(1)} %get-tuple-element.190), channel_id=1, source_target_pairs={{8,0},{16,8},{24,16},{9,1},{17,9},{25,17},{10,2},{18,10},{26,18},{... | collective-permute-start | bytes 393224 | tf_op jit(solution)/shard_map/ppermute | solution.py:20
  21.5 7.2 %collective-permute-start.2 = (f32[2,4,20,2,128]{4,2,3,1,0:T(8,128)}, f32[2,4,20,2,128]{4,2,3,1,0:T(8,128)S(1)}, u32[]{:S(2)}, u32[]{:S(2)}) collective-permute-start(f32[2,4,20,2,128]{4,2,3,1,0:T(8,128)} %get-tuple-element.185), channel_id=1, source_target_pairs={{0,4},{1,5},{2,6},{3,7},{8,12},{9,13},{10,14},{11,15},{16,20},{17,... | collective-permute-start | bytes 491528 | tf_op jit(solution)/shard_map/ppermute | solution.py:18
  24.9 7.7 %collective-permute-start.3 = (f32[2,4,20,2,128]{4,2,3,1,0:T(8,128)S(1)}, f32[2,4,20,2,128]{4,2,3,1,0:T(8,128)}, u32[]{:S(2)}, u32[]{:S(2)}) collective-permute-start(f32[2,4,20,2,128]{4,2,3,1,0:T(8,128)S(1)} %get-tuple-element.186), channel_id=1, source_target_pairs={{4,0},{5,1},{6,2},{7,3},{12,8},{13,9},{14,10},{15,11},{20,16},{21,... | collective-permute-start | bytes 491528 | tf_op jit(solution)/shard_map/ppermute | solution.py:20
  28.7 1.2 copy-start.2
  39.7 9.7 %collective-permute-start.4 = (f32[2,4,20,20,2]{3,2,4,1,0:T(8,128)}, f32[2,4,20,20,2]{3,2,4,1,0:T(8,128)}, u32[]{:S(2)}, u32[]{:S(2)}) collective-permute-start(f32[2,4,20,20,2]{3,2,4,1,0:T(8,128)} %copy.22), channel_id=1, source_target_pairs={{0,1},{1,2},{2,3},{4,5},{5,6},{6,7},{8,9},{9,10},{10,11},{12,13},{... | collective-permute-start | bytes 76808 | tf_op jit(solution)/shard_map/ppermute | solution.py:18
  45.1 7.8 %collective-permute-start.5 = (f32[2,4,20,20,2]{3,2,4,1,0:T(8,128)}, f32[2,4,20,20,2]{3,2,4,1,0:T(8,128)}, u32[]{:S(2)}, u32[]{:S(2)}) collective-permute-start(f32[2,4,20,20,2]{3,2,4,1,0:T(8,128)} %copy.24), channel_id=1, source_target_pairs={{1,0},{2,1},{3,2},{5,4},{6,5},{7,6},{9,8},{10,9},{11,10},{13,12},{... | collective-permute-start | bytes 76808 | tf_op jit(solution)/shard_map/ppermute | solution.py:20
  70.3 1.5 copy-start
  70.3 2.0 copy-start.1
  70.3 2.5 %copy-start.3 = (f32[2,4,18,16,128]{4,2,3,1,0:T(8,128)S(1)}, f32[2,4,18,16,128]{4,2,3,1,0:T(8,128)}, u32[]{:S(2)}) copy-start(f32[2,4,18,16,128]{4,2,3,1,0:T(8,128)} %copy-done.2) | copy-start | bytes 3538948
  77.5 0.9 copy-start.4
  78.4 67.7 %copy-start.5 = (s32[256]{0:T(256)S(1)}, s32[256]{0:T(256)}, u32[]{:S(2)}) copy-start(s32[256]{0:T(256)} %param.9) | copy-start | bytes 3076
Sparse Core Ops, SparseCore 0:
  160.7 33.8 reduce-scatter.3
where the time goes:
time: 205 us; the launch traced here: 203 us
  local copies, waits for them, and re-layouts  50.8 us (25%)
  waiting for transfers between devices  40.9 us (20%)
  loops' own time  31.3 us (15%)
  other arithmetic  25.1 us (12%)
  between operations  14.3 us (7%)
  starting transfers between devices  14.2 us (7%)
  blocking collectives  13.4 us (7%)
  matrix products  12.8 us (6%)
    unnamed x2, waiting for transfers between devices  32.7 us
    another operation x1, loops' own time, body(): lax.scan(bin_plane, jnp.zeros((steps_count, shell_count), jnp.float32), (...  31.3 us
    dynamic_slice x32, local copies, waits for them, and re-layouts, body(): lax.scan(bin_plane, jnp.zeros((steps_count, shell_count), jnp.float32), (...  23.1 us
    all_gather x1, blocking collectives, entering(): everything = lax.all_gather(value, axis)  13.4 us
    dot_general x16, matrix products, bin_plane(): jnp.dot(flux_piece, one_hot, precision=lax.Precision.HIGHEST)  12.8 us
    unnamed x17, local copies, waits for them, and re-layouts  10.3 us
    ppermute x3, starting transfers between devices, extended(): lax.ppermute(tail, axis, [(i, (i + 1) % count) for i in range(ends)])  10.3 us
    concatenate x3, other arithmetic, extended(): jnp.concatenate([lax.ppermute(tail, axis, [(i, (i + 1) % count) for i in...  10 us
  transfers between devices with their start and end apart: 7, of which 4 were waited for; matrix products, arithmetic and copies ran while one was open for 7% of the time, Pallas kernels for 0%

commit v1 on v0

v1 whole, which is shorter than its diff:
```python
import functools

import jax
import jax.numpy as jnp
from jax import lax
from jax.experimental import pallas as pl
from jax.experimental.pallas import tpu as pltpu
from jax.sharding import PartitionSpec as P

MESH = pl.DeviceIdType.MESH
HI = 8


def step(sizes, strain, cells, onset, psi_out, energy, grid, index, psi, edges, ends, halo_z,
         rows_out, rows_low, rows_high, first_z, parts, acc, table, inbox, carry, slabs,
         load_sem, out_sem, send_x, recv_x, send_y, recv_y, send_z, recv_z,
         send_bin, recv_bin, send_acc, recv_acc):
    ngx, ngy, ngz, steps, cx, cy, cz, shells = sizes
    fields = 2 * steps
    n_lo = shells // HI
    peers = ngy * ngz
    own = shells // peers
    gx, gy, gz = lax.axis_index("gx"), lax.axis_index("gy"), lax.axis_index("gz")
    rank = gy * ngz + gz

    load = pltpu.make_async_copy(strain, grid.at[:, pl.ds(2, cx), pl.ds(8, cy), :], load_sem.at[0])
    load.start()
    load_index = pltpu.make_async_copy(cells, index, load_sem.at[1])
    load_index.start()

    barrier = pltpu.get_barrier_semaphore()

    def greet_slab(k, _):
        q = lax.rem(rank + k, peers)
        pl.semaphore_signal(barrier, inc=1, device_id=(gx, q // ngz, lax.rem(q, ngz)), device_id_type=MESH)
        return 0

    def greet_line(k, _):
        pl.semaphore_signal(barrier, inc=1, device_id=(lax.rem(gx + k, ngx), gy, gz), device_id_type=MESH)
        return 0

    lax.fori_loop(1, ngx, greet_line, 0)
    lax.fori_loop(1, peers, greet_slab, 0)
    load.wait()

    lane = lax.broadcasted_iota(jnp.int32, (8, cz), 1)
    row = lax.broadcasted_iota(jnp.int32, (8, cz), 0)
    slot_of_lane = lane // 4

    for f in range(fields):
        packed = jnp.zeros((8, cz), jnp.float32)
        for x in range(cx):
            rows_out[0, pl.ds(f * 2 * cx + 2 * x, 2), :] = grid[f, x + 2, pl.ds(8, 2), :]
            rows_out[1, pl.ds(f * 2 * cx + 2 * x, 2), :] = grid[f, x + 2, pl.ds(6 + cy, 2), :]
            for half in range(2):
                slot = 2 * x + half
                moved = pltpu.roll(grid[f, x + 2, pl.ds(8 + 8 * half, 8), :], (2 + 4 * slot) % cz, 1)
                packed = jnp.where(slot_of_lane == slot, moved, packed)
        edges[f] = packed

    pl.semaphore_wait(barrier, peers - 1 + ngx - 1)

    def x_copy(side):
        there = gx + 1 if side == 0 else gx - 1
        return pltpu.make_async_remote_copy(
            src_ref=grid.at[:, pl.ds(cx if side == 0 else 2, 2), pl.ds(8, cy), :],
            dst_ref=grid.at[:, pl.ds(0 if side == 0 else cx + 2, 2), pl.ds(8, cy), :],
            send_sem=send_x.at[side], recv_sem=recv_x.at[side],
            device_id=(there, gy, gz), device_id_type=MESH)

    def y_copy(side):
        there = gy + 1 if side == 0 else gy - 1
        return pltpu.make_async_remote_copy(
            src_ref=rows_out.at[1 - side],
            dst_ref=(rows_low.at[pl.ds(8, fields * 2 * cx), :] if side == 0
                     else rows_high.at[pl.ds(0, fields * 2 * cx), :]),
            send_sem=send_y.at[side], recv_sem=recv_y.at[side],
            device_id=(gx, there, gz), device_id_type=MESH)

    def z_copy(side, dy):
        there = gz + 1 if side == 0 else gz - 1
        return pltpu.make_async_remote_copy(
            src_ref=edges, dst_ref=ends.at[side, 1 - dy],
            send_sem=send_z.at[side, 1 - dy], recv_sem=recv_z.at[side, 1 - dy],
            device_id=(gx, gy + dy, there), device_id_type=MESH)

    sends = ([gz < ngz - 1, gz > 0], [gy < ngy - 1, gy > 0], [gx < ngx - 1, gx > 0])
    gets = ([gz > 0, gz < ngz - 1], [gy > 0, gy < ngy - 1], [gx > 0, gx < ngx - 1])
    near = {-1: gy > 0, 0: gy >= 0, 1: gy < ngy - 1}

    for side in range(2):
        for dy in (0, -1, 1):
            @pl.when(jnp.logical_and(sends[0][side], near[dy]))
            def _(side=side, dy=dy):
                z_copy(side, dy).start()
    for side in range(2):
        @pl.when(sends[1][side])
        def _(side=side):
            y_copy(side).start()
    for side in range(2):
        @pl.when(sends[2][side])
        def _(side=side):
            x_copy(side).start()

    for side in range(2):
        for dy in (-1, 0, 1):
            @pl.when(jnp.logical_not(jnp.logical_and(gets[0][side], near[dy])))
            def _(side=side, dy=dy):
                ends[side, 1 + dy] = jnp.zeros(ends.shape[2:], jnp.float32)

        @pl.when(jnp.logical_not(gets[2][side]))
        def _(side=side):
            grid[:, pl.ds(0 if side == 0 else cx + 2, 2), pl.ds(8, cy), :] = jnp.zeros(
                (fields, 2, cy, cz), jnp.float32)

    @pl.when(jnp.logical_not(gets[1][0]))
    def _():
        rows_low[...] = jnp.zeros(rows_low.shape, jnp.float32)

    @pl.when(jnp.logical_not(gets[1][1]))
    def _():
        rows_high[...] = jnp.zeros(rows_high.shape, jnp.float32)

    acc[...] = jnp.zeros(acc.shape, jnp.float32)
    table[...] = jnp.zeros(table.shape, jnp.float32)
    load_index.wait()

    for side in range(2):
        for dy in (0, -1, 1):
            @pl.when(jnp.logical_and(gets[0][side], near[dy]))
            def _(side=side, dy=dy):
                z_copy(side, -dy).wait_recv()

    from_left = lax.rem(lane, 4) < 2
    for f in range(fields):
        halo_z[0, f] = jnp.where(from_left, ends[0, 1, f], ends[1, 1, f])
        low = jnp.where(from_left, ends[0, 0, f], ends[1, 0, f])
        high = jnp.where(from_left, ends[0, 2, f], ends[1, 2, f])
        halo_z[1, f] = jnp.where(row < 4, pltpu.roll(high, 4, 1), low)

    for side in range(2):
        @pl.when(gets[1][side])
        def _(side=side):
            y_copy(side).wait_recv()

    wide = lax.broadcasted_iota(jnp.int32, (cy, cz), 0)
    far = lax.broadcasted_iota(jnp.int32, (cy, cz), 1)
    uy = ((gy * cy + wide).astype(jnp.float32) + 0.5) / (cy * ngy) - 0.5
    uz = ((gz * cz + far).astype(jnp.float32) + 0.5) / (cz * ngz) - 0.5
    rsq_yz = uy * uy + uz * uz + 0.05
    low_label = lax.broadcasted_iota(jnp.int32, (n_lo, cz), 0)
    head, tail = lane < 2, lane >= cz - 2

    def along(cell, halo, shift):
        ring = pltpu.roll(halo, shift, 1)
        m2 = pltpu.roll(jnp.where(tail, ring, cell), 2, 1)
        m1 = pltpu.roll(jnp.where(lane == cz - 1, ring, cell), 1, 1)
        p1 = pltpu.roll(jnp.where(lane == 0, ring, cell), cz - 1, 1)
        p2 = pltpu.roll(jnp.where(head, ring, cell), cz - 2, 1)
        return m2, m1, p1, p2

    def plane(i, _):
        x = lax.rem(i + 2, cx)

        @pl.when(i == cx - 4)
        def _():
            for side in range(2):
                @pl.when(gets[2][side])
                def _(side=side):
                    x_copy(side).wait_recv()

        shift0 = lax.rem(2 * cz - 2 - 8 * x, cz)
        shift1 = lax.rem(2 * cz - 6 - 8 * x, cz)
        combo, mixed = [], []
        for f in range(fields):
            base = f * 2 * cx + 2 * x
            outside = jnp.where(row < 4, rows_high[pl.ds(base, 8), :], rows_low[pl.ds(base + 2, 8), :])
            grid[f, x + 2, pl.ds(0, 8), :] = outside
            grid[f, x + 2, pl.ds(8 + cy, 8), :] = outside
            m2, m1, p1, p2 = along(outside, halo_z[1, f], shift1)
            d = 8.0 * (p1 - m1) - (p2 - m2)
            first_z[f, pl.ds(0, 8), :] = d
            first_z[f, pl.ds(8 + cy, 8), :] = d
            seconds = []
            for half in range(2):
                cell = grid[f, x + 2, pl.ds(8 + 8 * half, 8), :]
                m2, m1, p1, p2 = along(cell, halo_z[0, f], shift1 if half else shift0)
                first_z[f, pl.ds(8 + 8 * half, 8), :] = 8.0 * (p1 - m1) - (p2 - m2)
                seconds.append(16.0 * (p1 + m1) - (p2 + m2))
            center = grid[f, x + 2, pl.ds(8, cy), :]
            near_xy = (grid[f, x + 1, pl.ds(8, cy), :] + grid[f, x + 3, pl.ds(8, cy), :]
                       + grid[f, x + 2, pl.ds(7, cy), :] + grid[f, x + 2, pl.ds(9, cy), :])
            far_xy = (grid[f, x, pl.ds(8, cy), :] + grid[f, x + 4, pl.ds(8, cy), :]
                      + grid[f, x + 2, pl.ds(6, cy), :] + grid[f, x + 2, pl.ds(10, cy), :])
            combo.append(16.0 * near_xy - far_xy - 30.0 * center - jnp.concatenate(seconds, 0))
            mixed.append(8.0 * (first_z[f, pl.ds(9, cy), :] - first_z[f, pl.ds(7, cy), :])
                         - (first_z[f, pl.ds(10, cy), :] - first_z[f, pl.ds(6, cy), :]))
        ux = ((gx * cx + x).astype(jnp.float32) + 0.5) * (1.0 / (cx * ngx)) - 0.5
        rsq = (rsq_yz + ux * ux) * 0.0625
        news_re = jnp.zeros((cy, cz), jnp.float32)
        news_im = jnp.zeros((cy, cz), jnp.float32)
        for t in range(steps):
            re = combo[t] * (1.0 / 24.0) - mixed[steps + t] * (1.0 / 144.0)
            im = combo[steps + t] * (-1.0 / 24.0) - mixed[t] * (1.0 / 144.0)
            psi[t, x] = re
            psi[steps + t, x] = im
            news_re, news_im = news_re + re, news_im + im
            flux = rsq * (news_re * news_re + news_im * news_im)
            coarse = flux.astype(jnp.bfloat16).astype(jnp.float32)
            parts[2 * t] = coarse
            parts[2 * t + 1] = flux - coarse
        pltpu.make_async_copy(psi.at[:, x], psi_out.at[:, x], out_sem.at[x]).start()

        total = acc[...]
        group = 4
        for y0 in range(0, cy, group):
            left, right = [], []
            hit = []
            for y in range(y0, y0 + group):
                shell = index[x, pl.ds(y, 1), :]
                high = shell // n_lo
                low = shell - high * n_lo
                hit.append(jnp.broadcast_to(high, (HI, cz)) == row)
                right.append(jnp.where(jnp.broadcast_to(low, (n_lo, cz)) == low_label, 1.0, 0.0))
            for p in range(2 * steps):
                left.append(jnp.concatenate(
                    [jnp.where(hit[k], jnp.broadcast_to(parts[p, pl.ds(y0 + k, 1), :], (HI, cz)), 0.0)
                     for k in range(group)], 1))
            total = total + lax.dot_general(
                jnp.concatenate(left, 0).astype(jnp.bfloat16),
                jnp.concatenate(right, 1).astype(jnp.bfloat16),
                (((1,), (1,)), ((), ())), preferred_element_type=jnp.float32)
        acc[...] = total
        return 0

    lax.fori_loop(0, cx, plane, 0)

    for t in range(steps):
        both = acc[pl.ds(16 * t, 8), :] + acc[pl.ds(16 * t + 8, 8), :]
        for h in range(HI):
            table[h, pl.ds(t, 1), pl.ds(0, n_lo)] = both[h:h + 1, :]

    spread = peers // HI

    def bin_copy(k):
        q = lax.rem(rank + k, peers)
        return pltpu.make_async_remote_copy(
            src_ref=table.at[q // spread], dst_ref=inbox.at[rank],
            send_sem=send_bin.at[k], recv_sem=recv_bin.at[rank],
            device_id=(gx, q // ngz, lax.rem(q, ngz)), device_id_type=MESH)

    def bin_arrival(k):
        q = lax.rem(rank + k, peers)
        return pltpu.make_async_remote_copy(
            src_ref=table.at[0], dst_ref=inbox.at[q],
            send_sem=send_bin.at[k], recv_sem=recv_bin.at[q],
            device_id=(gx, q // ngz, lax.rem(q, ngz)), device_id_type=MESH)

    def send_one(k, _):
        bin_copy(k).start()
        return 0

    lax.fori_loop(1, peers, send_one, 0)

    def take_one(k, total):
        bin_arrival(k).wait_recv()
        return total + inbox[lax.rem(rank + k, peers)]

    total = lax.fori_loop(1, peers, take_one, table[rank // spread])
    first = rank * own
    labels = jnp.zeros((8, 128), jnp.int32)
    for block in range(shells // 128):
        piece = jnp.broadcast_to(onset[:, pl.ds(block * 128, 128)], (8, 128))
        labels = jnp.where(first // 128 == block, piece, labels)
    labels = pltpu.roll(labels, lax.rem(128 - lax.rem(first, 128), 128), 1)
    total = pltpu.roll(total, lax.rem(128 - lax.rem(rank, spread) * own, 128), 1)
    total = jnp.where(row >= labels, total, 0.0)
    scale = 0.25 * shells / (cx * ngx * cy * ngy * cz * ngz)
    running = jnp.zeros((1, 128), jnp.float32)
    sums = []
    for t in range(steps):
        running = running + total[t:t + 1, :]
        sums.append(running * scale)
    sums.append(jnp.zeros((8 - steps, 128), jnp.float32))
    mine = jnp.concatenate(sums, 0)
    carry[...] = mine

    def line_copy(there):
        return pltpu.make_async_remote_copy(
            src_ref=carry, dst_ref=slabs.at[gx],
            send_sem=send_acc.at[there], recv_sem=recv_acc.at[gx],
            device_id=(there, gy, gz), device_id_type=MESH)

    def line_arrival(h):
        return pltpu.make_async_remote_copy(
            src_ref=carry, dst_ref=slabs.at[h],
            send_sem=send_acc.at[h], recv_sem=recv_acc.at[h],
            device_id=(h, gy, gz), device_id_type=MESH)

    def send_line(k, _):
        line_copy(gx + k).start()
        return 0

    lax.fori_loop(1, ngx - gx, send_line, 0)

    def take_line(h, total):
        line_arrival(h).wait_recv()
        return total + slabs[h]

    energy[...] = lax.fori_loop(0, gx, take_line, mine)[:steps, :own]

    def end_out(x, _):
        pltpu.make_async_copy(psi.at[:, x], psi_out.at[:, x], out_sem.at[x]).wait()
        return 0

    lax.fori_loop(0, cx, end_out, 0)

    for side in range(2):
        for dy in (0, -1, 1):
            @pl.when(jnp.logical_and(sends[0][side], near[dy]))
            def _(side=side, dy=dy):
                z_copy(side, dy).wait_send()

        @pl.when(sends[1][side])
        def _(side=side):
            y_copy(side).wait_send()

        @pl.when(sends[2][side])
        def _(side=side):
            x_copy(side).wait_send()

    def end_one(k, _):
        bin_copy(k).wait_send()
        return 0

    lax.fori_loop(1, peers, end_one, 0)

    def end_line(k, _):
        line_copy(gx + k).wait_send()
        return 0

    lax.fori_loop(1, ngx - gx, end_line, 0)


def body(strain, cell_shell_index, onset_step):
    comps, steps, cx, cy, cz = strain.shape
    shells = onset_step.shape[0]
    ngx, ngy, ngz = lax.axis_size("gx"), lax.axis_size("gy"), lax.axis_size("gz")
    peers = ngy * ngz
    own = shells // peers
    fields = comps * steps
    n_lo = shells // HI
    f32 = jnp.float32
    dma = pltpu.SemaphoreType.DMA
    sizes = (ngx, ngy, ngz, steps, cx, cy, cz, shells)
    anywhere = pl.BlockSpec(memory_space=pl.ANY)
    vmem = pl.BlockSpec(memory_space=pltpu.VMEM)
    psi, energy = pl.pallas_call(
        functools.partial(step, sizes),
        out_shape=(
            jax.ShapeDtypeStruct((fields, cx, cy, cz), f32),
            jax.ShapeDtypeStruct((steps, own), f32),
        ),
        in_specs=[anywhere, anywhere, vmem],
        out_specs=(anywhere, vmem),
        scratch_shapes=[
            pltpu.VMEM((fields, cx + 4, cy + 16, cz), f32),
            pltpu.VMEM((cx, cy, cz), jnp.int32),
            pltpu.VMEM((fields, cx, cy, cz), f32),
            pltpu.VMEM((fields, 8, cz), f32),
            pltpu.VMEM((2, 3, fields, 8, cz), f32),
            pltpu.VMEM((2, fields, 8, cz), f32),
            pltpu.VMEM((2, fields * 2 * cx, cz), f32),
            pltpu.VMEM((fields * 2 * cx + 8, cz), f32),
            pltpu.VMEM((fields * 2 * cx + 8, cz), f32),
            pltpu.VMEM((fields, cy + 16, cz), f32),
            pltpu.VMEM((2 * steps, cy, cz), f32),
            pltpu.VMEM((2 * steps * HI, n_lo), f32),
            pltpu.VMEM((HI, 8, 128), f32),
            pltpu.VMEM((peers, 8, 128), f32),
            pltpu.VMEM((8, 128), f32),
            pltpu.VMEM((ngx, 8, 128), f32),
            dma((2,)), dma((cx,)),
            dma((2,)), dma((2,)), dma((2,)), dma((2,)), dma((2, 3)), dma((2, 3)),
            dma((peers,)), dma((peers,)), dma((ngx,)), dma((ngx,)),
        ],
        compiler_params=pltpu.CompilerParams(
            collective_id=0, has_side_effects=True, vmem_limit_bytes=32 * 1024 * 1024),
    )(strain.reshape(fields, cx, cy, cz), cell_shell_index, onset_step.reshape(1, shells))
    return psi.reshape(strain.shape), energy[None]


def solution(mesh):
    placed = (P(None, None, "gx", "gy", "gz"), P("gx", "gy", "gz"), P())
    return jax.shard_map(
        body,
        mesh=mesh,
        in_specs=placed,
        out_specs=(P(None, None, "gx", "gy", "gz"), P("gx", None, ("gy", "gz"))),
        check_vma=False,
    )
```

time: 205 us -> 29.9 us (0.15)
  local copies, waits for them, and re-layouts: 50.8 us -> 4.35 us
  waiting for transfers between devices: 40.9 us -> 0 us
  loops' own time: 31.3 us -> 0 us
  other arithmetic: 25.1 us -> 0 us
  Pallas kernels: 0 us -> 24.7 us
  starting transfers between devices: 14.2 us -> 0 us
  between operations: 14.3 us -> 0.65 us
  blocking collectives: 13.4 us -> 0 us
  matrix products: 12.8 us -> 0 us
    unnamed x2 -> x0, waiting for transfers between devices: 32.7 us -> none
    another operation x2 -> x0, loops' own time: 31.3 us -> none  [the longest x1 31.3 us: body(): lax.scan(bin_plane, jnp.zeros((steps_count, shell_count), jnp.float32), (...]
    pallas_call x0 -> x1, Pallas kernels: none -> 24.7 us  [body(): pl.pallas_call(functools.partial(step, sizes), out_shape=(jax.ShapeDtypeS...]
    dynamic_slice x48 -> x0, local copies, waits for them, and re-layouts: 23.6 us -> none  [the longest x32 23.1 us: body(): lax.scan(bin_plane, jnp.zeros((steps_count, shell_count), jnp.float32), (...]
    ppermute x6 -> x0, starting transfers between devices: 14.2 us -> none  [the longest x3 10.3 us: extended(): lax.ppermute(tail, axis, [(i, (i + 1) % count) for i in range(ends)])]
    all_gather x1 -> x0, blocking collectives: 13.4 us -> none  [entering(): everything = lax.all_gather(value, axis)]
    dot_general x16 -> x0, matrix products: 12.8 us -> none  [bin_plane(): jnp.dot(flux_piece, one_hot, precision=lax.Precision.HIGHEST)]
    concatenate x3 -> x0, other arithmetic: 10 us -> none  [extended(): jnp.concatenate([lax.ppermute(tail, axis, [(i, (i + 1) % count) for i in...]
  transfers between devices with their start and end apart: 7 -> 0, of which waited for: 4 -> 0; matrix products, arithmetic and copies ran while one was open for 7% -> 0% of each run, Pallas kernels for 0% -> 0%
where the time goes in v1:
time: 29.9 us; the launch traced here: 29.7 us
  Pallas kernels  24.7 us (83%)
  local copies, waits for them, and re-layouts  4.35 us (15%)
  between operations  0.65 us (2%)
    pallas_call x1, Pallas kernels, body(): pl.pallas_call(functools.partial(step, sizes), out_shape=(jax.ShapeDtypeS...  24.7 us
    unnamed x8, local copies, waits for them, and re-layouts  4.35 us

profile of v1, /device:TPU:0, one launch (start us, length us, event | category | flops | bytes accessed | tf_op | source)
XLA Modules:
  0.0 29.7 jit_solution(16905014375427776884)
XLA Ops:
  0.6 0.0 copy-start.2
  0.6 0.7 %copy-done.2 = s32[256]{0:T(256)S(1)} copy-done((s32[256]{0:T(256)S(1)}, s32[256]{0:T(256)}, u32[]{:S(2)}) %copy-start.2) | copy-done | bytes 1048
  1.3 0.0 copy-start
  1.3 1.2 %copy-done = f32[2,4,16,16,128]{4,3,2,1,0:T(8,128)S(1)} copy-done((f32[2,4,16,16,128]{4,3,2,1,0:T(8,128)S(1)}, f32[2,4,16,16,128]{4,3,2,1,0:T(8,128)}, u32[]{:S(2)}) %copy-start) | copy-done | bytes 1048600
  2.5 0.0 copy-start.1
  2.5 0.9 %copy-done.1 = s32[16,16,128]{2,1,0:T(8,128)S(1)} copy-done((s32[16,16,128]{2,1,0:T(8,128)S(1)}, s32[16,16,128]{2,1,0:T(8,128)}, u32[]{:S(2)}) %copy-start.1) | copy-done | bytes 131096
  3.4 24.7 %shard_map.50 = (f32[8,16,16,128]{3,2,1,0:T(8,128)S(1)}, f32[4,32]{1,0:T(4,128)S(1)}) custom-call(f32[8,16,16,128]{3,2,1,0:T(8,128)S(1)} %bitcast.4, s32[16,16,128]{2,1,0:T(8,128)S(1)} %copy-done.1, s32[1,256]{1,0:T(1,128)S(1)} %bitcast.7), custom_call_target="tpu_custom_call" | custom-call | tf_op jit(solution)/shard_map/pallas_call | solution.py:358
  28.1 1.0 %copy.7 = f32[2,4,16,16,128]{4,3,2,1,0:T(8,128)} copy(f32[2,4,16,16,128]{4,3,2,1,0:T(8,128)S(1)} %bitcast.5) | data formatting | bytes 2097152
  29.1 0.6 %copy.8 = f32[1,4,32]{2,1,0:T(4,128)} copy(f32[1,4,32]{2,1,0:T(4,128)S(1)} %bitcast.6) | data formatting | bytes 1024
Async XLA Ops:
  0.6 0.7 %copy-start.2 = (s32[256]{0:T(256)S(1)}, s32[256]{0:T(256)}, u32[]{:S(2)}) copy-start(s32[256]{0:T(256)} %param.5) | copy-start | bytes 3076
  1.3 1.2 %copy-start = (f32[2,4,16,16,128]{4,3,2,1,0:T(8,128)S(1)}, f32[2,4,16,16,128]{4,3,2,1,0:T(8,128)}, u32[]{:S(2)}) copy-start(f32[2,4,16,16,128]{4,3,2,1,0:T(8,128)} %param.3) | copy-start | bytes 3145732
  2.5 0.9 %copy-start.1 = (s32[16,16,128]{2,1,0:T(8,128)S(1)}, s32[16,16,128]{2,1,0:T(8,128)}, u32[]{:S(2)}) copy-start(s32[16,16,128]{2,1,0:T(8,128)} %cells.1) | copy-start | bytes 393220

commit v2 on v1

--- a/solution.py
+++ b/solution.py
@@ -11,7 +11,7 @@
 HI = 8
 
 
-def step(sizes, strain, cells, onset, psi_out, energy, grid, index, psi, edges, ends, halo_z,
+def step(sizes, strain, cells, onset, psi_out, energy, grid, index, psi, edges, ends, halo_z, corners, corner_in, slope_low, slope_high,
          rows_out, rows_low, rows_high, first_z, parts, acc, table, inbox, carry, slabs,
          load_sem, out_sem, send_x, recv_x, send_y, recv_y, send_z, recv_z,
          send_bin, recv_bin, send_acc, recv_acc):
@@ -58,6 +58,13 @@
                 packed = jnp.where(slot_of_lane == slot, moved, packed)
         edges[f] = packed
 
+    for side in range(2):
+        packed = jnp.zeros((8, cz), jnp.float32)
+        for slot in range(fields * cx // 4):
+            moved = pltpu.roll(rows_out[side, pl.ds(8 * slot, 8), :], (2 + 4 * slot) % cz, 1)
+            packed = jnp.where(slot_of_lane == slot, moved, packed)
+        corners[side] = packed
+
     pl.semaphore_wait(barrier, peers - 1 + ngx - 1)
 
     def x_copy(side):
@@ -80,7 +87,8 @@
     def z_copy(side, dy):
         there = gz + 1 if side == 0 else gz - 1
         return pltpu.make_async_remote_copy(
-            src_ref=edges, dst_ref=ends.at[side, 1 - dy],
+            src_ref=edges if dy == 0 else corners.at[0 if dy < 0 else 1],
+            dst_ref=ends.at[side] if dy == 0 else corner_in.at[side, 0 if dy > 0 else 1],
             send_sem=send_z.at[side, 1 - dy], recv_sem=recv_z.at[side, 1 - dy],
             device_id=(gx, gy + dy, there), device_id_type=MESH)
 
@@ -106,7 +114,10 @@
         for dy in (-1, 0, 1):
             @pl.when(jnp.logical_not(jnp.logical_and(gets[0][side], near[dy])))
             def _(side=side, dy=dy):
-                ends[side, 1 + dy] = jnp.zeros(ends.shape[2:], jnp.float32)
+                if dy == 0:
+                    ends[side] = jnp.zeros(ends.shape[1:], jnp.float32)
+                else:
+                    corner_in[side, 0 if dy < 0 else 1] = jnp.zeros((8, cz), jnp.float32)
 
         @pl.when(jnp.logical_not(gets[2][side]))
         def _(side=side):
@@ -133,10 +144,7 @@
 
     from_left = lax.rem(lane, 4) < 2
     for f in range(fields):
-        halo_z[0, f] = jnp.where(from_left, ends[0, 1, f], ends[1, 1, f])
-        low = jnp.where(from_left, ends[0, 0, f], ends[1, 0, f])
-        high = jnp.where(from_left, ends[0, 2, f], ends[1, 2, f])
-        halo_z[1, f] = jnp.where(row < 4, pltpu.roll(high, 4, 1), low)
+        halo_z[f] = jnp.where(from_left, ends[0, f], ends[1, f])
 
     for side in range(2):
         @pl.when(gets[1][side])
@@ -158,6 +166,19 @@
         p1 = pltpu.roll(jnp.where(lane == 0, ring, cell), cz - 1, 1)
         p2 = pltpu.roll(jnp.where(head, ring, cell), cz - 2, 1)
         return m2, m1, p1, p2
+
+    for end, (rows, first, slope) in enumerate(((rows_low, 8, slope_low), (rows_high, 0, slope_high))):
+        @pl.when(gets[1][end])
+        def _(end=end, rows=rows, first=first, slope=slope):
+            ring = jnp.where(from_left, corner_in[0, end], corner_in[1, end])
+            for slot in range(fields * cx // 4):
+                m2, m1, p1, p2 = along(rows[pl.ds(first + 8 * slot, 8), :], ring, (2 * cz - 2 - 4 * slot) % cz)
+                slope[pl.ds(first + 8 * slot, 8), :] = 8.0 * (p1 - m1) - (p2 - m2)
+
+        @pl.when(jnp.logical_not(gets[1][end]))
+        def _(slope=slope):
+            slope[...] = jnp.zeros(slope.shape, jnp.float32)
+
 
     def plane(i, _):
         x = lax.rem(i + 2, cx)
@@ -177,14 +198,13 @@
             outside = jnp.where(row < 4, rows_high[pl.ds(base, 8), :], rows_low[pl.ds(base + 2, 8), :])
             grid[f, x + 2, pl.ds(0, 8), :] = outside
             grid[f, x + 2, pl.ds(8 + cy, 8), :] = outside
-            m2, m1, p1, p2 = along(outside, halo_z[1, f], shift1)
-            d = 8.0 * (p1 - m1) - (p2 - m2)
+            d = jnp.where(row < 4, slope_high[pl.ds(base, 8), :], slope_low[pl.ds(base + 2, 8), :])
             first_z[f, pl.ds(0, 8), :] = d
             first_z[f, pl.ds(8 + cy, 8), :] = d
             seconds = []
             for half in range(2):
                 cell = grid[f, x + 2, pl.ds(8 + 8 * half, 8), :]
-                m2, m1, p1, p2 = along(cell, halo_z[0, f], shift1 if half else shift0)
+                m2, m1, p1, p2 = along(cell, halo_z[f], shift1 if half else shift0)
                 first_z[f, pl.ds(8 + 8 * half, 8), :] = 8.0 * (p1 - m1) - (p2 - m2)
                 seconds.append(16.0 * (p1 + m1) - (p2 + m2))
             center = grid[f, x + 2, pl.ds(8, cy), :]
@@ -353,7 +373,7 @@
     f32 = jnp.float32
     dma = pltpu.SemaphoreType.DMA
     sizes = (ngx, ngy, ngz, steps, cx, cy, cz, shells)
-    anywhere = pl.BlockSpec(memory_space=pl.ANY)
+    anywhere = pl.BlockSpec(memory_space=pltpu.HBM)
     vmem = pl.BlockSpec(memory_space=pltpu.VMEM)
     psi, energy = pl.pallas_call(
         functools.partial(step, sizes),
@@ -368,8 +388,12 @@
             pltpu.VMEM((cx, cy, cz), jnp.int32),
             pltpu.VMEM((fields, cx, cy, cz), f32),
             pltpu.VMEM((fields, 8, cz), f32),
-            pltpu.VMEM((2, 3, fields, 8, cz), f32),
             pltpu.VMEM((2, fields, 8, cz), f32),
+            pltpu.VMEM((fields, 8, cz), f32),
+            pltpu.VMEM((2, 8, cz), f32),
+            pltpu.VMEM((2, 2, 8, cz), f32),
+            pltpu.VMEM((fields * 2 * cx + 8, cz), f32),
+            pltpu.VMEM((fields * 2 * cx + 8, cz), f32),
             pltpu.VMEM((2, fields * 2 * cx, cz), f32),
             pltpu.VMEM((fields * 2 * cx + 8, cz), f32),
             pltpu.VMEM((fields * 2 * cx + 8, cz), f32),
@@ -385,7 +409,7 @@
             dma((peers,)), dma((peers,)), dma((ngx,)), dma((ngx,)),
         ],
         compiler_params=pltpu.CompilerParams(
-            collective_id=0, has_side_effects=True, vmem_limit_bytes=32 * 1024 * 1024),
+            collective_id=0, has_side_effects=True, vmem_limit_bytes=67043328 - 512 * 1024),
     )(strain.reshape(fields, cx, cy, cz), cell_shell_index, onset_step.reshape(1, shells))
     return psi.reshape(strain.shape), energy[None]
 

time: 29.9 us -> 27.8 us (0.930)
  local copies, waits for them, and re-layouts: 4.35 us -> 2.85 us
  Pallas kernels: 24.7 us -> 24.1 us
    unnamed x8 -> x4, local copies, waits for them, and re-layouts: 4.35 us -> 2.85 us
    pallas_call x1, Pallas kernels: 24.7 us -> 24.1 us  [body(): pl.pallas_call(functools.partial(step, sizes), out_shape=(jax.ShapeDtypeS...]
where the time goes in v2:
time: 27.8 us; the launch traced here: 27.6 us
  Pallas kernels  24.1 us (87%)
  local copies, waits for them, and re-layouts  2.85 us (10%)
  between operations  0.65 us (2%)
    pallas_call x1, Pallas kernels, body(): pl.pallas_call(functools.partial(step, sizes), out_shape=(jax.ShapeDtypeS...  24.1 us
    unnamed x4, local copies, waits for them, and re-layouts  2.85 us

profile of v2, /device:TPU:0, one launch (start us, length us, event | category | flops | bytes accessed | tf_op | source)
XLA Modules:
  0.0 27.6 jit_solution(3509605202197859979)
XLA Ops:
  0.6 24.1 %shard_map.50 = (f32[8,16,16,128]{3,2,1,0:T(8,128)}, f32[4,32]{1,0:T(4,128)}) custom-call(f32[8,16,16,128]{3,2,1,0:T(8,128)} %bitcast.4, s32[16,16,128]{2,1,0:T(8,128)} %cells.1, s32[1,256]{1,0:T(1,128)} %bitcast.7), custom_call_target="tpu_custom_call" | custom-call | tf_op jit(solution)/shard_map/pallas_call | solution.py:378
  24.8 0.0 copy-start
  24.8 2.3 %copy.7 = f32[2,4,16,16,128]{4,3,2,1,0:T(8,128)} copy(f32[2,4,16,16,128]{4,3,2,1,0:T(8,128)} %bitcast.5) | data formatting | bytes 2097152
  27.1 0.0 copy-done
  27.1 0.6 %copy.8 = f32[1,4,32]{2,1,0:T(4,128)} copy(f32[1,4,32]{2,1,0:T(4,128)S(1)} %bitcast.6) | data formatting | bytes 1024
Async XLA Ops:
  24.8 2.3 %copy-start = (f32[4,32]{1,0:T(4,128)S(1)}, f32[4,32]{1,0:T(4,128)}, u32[]{:S(2)}) copy-start(f32[4,32]{1,0:T(4,128)} %get-tuple-element.5) | copy-start | bytes 1540

commit v3 on v2

--- a/solution.py
+++ b/solution.py
@@ -12,7 +12,7 @@
 
 
 def step(sizes, strain, cells, onset, psi_out, energy, grid, index, psi, edges, ends, halo_z, corners, corner_in, slope_low, slope_high,
-         rows_out, rows_low, rows_high, first_z, parts, acc, table, inbox, carry, slabs,
+         rows_out, rows_low, rows_high, first_z, some, parts, acc, table, inbox, carry, slabs,
          load_sem, out_sem, send_x, recv_x, send_y, recv_y, send_z, recv_z,
          send_bin, recv_bin, send_acc, recv_acc):
     ngx, ngy, ngz, steps, cx, cy, cz, shells = sizes
@@ -48,16 +48,54 @@
     slot_of_lane = lane // 4
 
     for f in range(fields):
-        packed = jnp.zeros((8, cz), jnp.float32)
         for x in range(cx):
             rows_out[0, pl.ds(f * 2 * cx + 2 * x, 2), :] = grid[f, x + 2, pl.ds(8, 2), :]
             rows_out[1, pl.ds(f * 2 * cx + 2 * x, 2), :] = grid[f, x + 2, pl.ds(6 + cy, 2), :]
+
+    pl.semaphore_wait(barrier, peers - 1 + ngx - 1)
+
+    def x_copy(side):
+        there = gx + 1 if side == 0 else gx - 1
+        return pltpu.make_async_remote_copy(
+            src_ref=grid.at[:, pl.ds(cx if side == 0 else 2, 2), pl.ds(8, cy), :],
+            dst_ref=grid.at[:, pl.ds(0 if side == 0 else cx + 2, 2), pl.ds(8, cy), :],
+            send_sem=send_x.at[side], recv_sem=recv_x.at[side],
+            device_id=(there, gy, gz), device_id_type=MESH)
+
+    def y_copy(side):
+        there = gy + 1 if side == 0 else gy - 1
+        return pltpu.make_async_remote_copy(
+            src_ref=rows_out.at[1 - side],
+            dst_ref=(rows_low.at[pl.ds(8, fields * 2 * cx), :] if side == 0
+                     else rows_high.at[pl.ds(0, fields * 2 * cx), :]),
+            send_sem=send_y.at[side], recv_sem=recv_y.at[side],
+            device_id=(gx, there, gz), device_id_type=MESH)
+
+    def z_copy(side, dy):
+        there = gz + 1 if side == 0 else gz - 1
+        return pltpu.make_async_remote_copy(
+            src_ref=edges if dy == 0 else corners.at[0 if dy < 0 else 1],
+            dst_ref=ends.at[side] if dy == 0 else corner_in.at[side, 0 if dy > 0 else 1],
+            send_sem=send_z.at[side, 1 - dy], recv_sem=recv_z.at[side, 1 - dy],
+            device_id=(gx, gy + dy, there), device_id_type=MESH)
+
+    sends = ([gz < ngz - 1, gz > 0], [gy < ngy - 1, gy > 0], [gx < ngx - 1, gx > 0])
+    gets = ([gz > 0, gz < ngz - 1], [gy > 0, gy < ngy - 1], [gx > 0, gx < ngx - 1])
+    near = {-1: gy > 0, 0: gy >= 0, 1: gy < ngy - 1}
+
+    for side in range(2):
+        @pl.when(sends[1][side])
+        def _(side=side):
+            y_copy(side).start()
+
+    for f in range(fields):
+        packed = jnp.zeros((8, cz), jnp.float32)
+        for x in range(cx):
             for half in range(2):
                 slot = 2 * x + half
                 moved = pltpu.roll(grid[f, x + 2, pl.ds(8 + 8 * half, 8), :], (2 + 4 * slot) % cz, 1)
                 packed = jnp.where(slot_of_lane == slot, moved, packed)
         edges[f] = packed
-
     for side in range(2):
         packed = jnp.zeros((8, cz), jnp.float32)
         for slot in range(fields * cx // 4):
@@ -65,50 +103,15 @@
             packed = jnp.where(slot_of_lane == slot, moved, packed)
         corners[side] = packed
 
-    pl.semaphore_wait(barrier, peers - 1 + ngx - 1)
-
-    def x_copy(side):
-        there = gx + 1 if side == 0 else gx - 1
-        return pltpu.make_async_remote_copy(
-            src_ref=grid.at[:, pl.ds(cx if side == 0 else 2, 2), pl.ds(8, cy), :],
-            dst_ref=grid.at[:, pl.ds(0 if side == 0 else cx + 2, 2), pl.ds(8, cy), :],
-            send_sem=send_x.at[side], recv_sem=recv_x.at[side],
-            device_id=(there, gy, gz), device_id_type=MESH)
-
-    def y_copy(side):
-        there = gy + 1 if side == 0 else gy - 1
-        return pltpu.make_async_remote_copy(
-            src_ref=rows_out.at[1 - side],
-            dst_ref=(rows_low.at[pl.ds(8, fields * 2 * cx), :] if side == 0
-                     else rows_high.at[pl.ds(0, fields * 2 * cx), :]),
-            send_sem=send_y.at[side], recv_sem=recv_y.at[side],
-            device_id=(gx, there, gz), device_id_type=MESH)
-
-    def z_copy(side, dy):
-        there = gz + 1 if side == 0 else gz - 1
-        return pltpu.make_async_remote_copy(
-            src_ref=edges if dy == 0 else corners.at[0 if dy < 0 else 1],
-            dst_ref=ends.at[side] if dy == 0 else corner_in.at[side, 0 if dy > 0 else 1],
-            send_sem=send_z.at[side, 1 - dy], recv_sem=recv_z.at[side, 1 - dy],
-            device_id=(gx, gy + dy, there), device_id_type=MESH)
-
-    sends = ([gz < ngz - 1, gz > 0], [gy < ngy - 1, gy > 0], [gx < ngx - 1, gx > 0])
-    gets = ([gz > 0, gz < ngz - 1], [gy > 0, gy < ngy - 1], [gx > 0, gx < ngx - 1])
-    near = {-1: gy > 0, 0: gy >= 0, 1: gy < ngy - 1}
-
+    for side in range(2):
+        @pl.when(sends[2][side])
+        def _(side=side):
+            x_copy(side).start()
     for side in range(2):
         for dy in (0, -1, 1):
             @pl.when(jnp.logical_and(sends[0][side], near[dy]))
             def _(side=side, dy=dy):
                 z_copy(side, dy).start()
-    for side in range(2):
-        @pl.when(sends[1][side])
-        def _(side=side):
-            y_copy(side).start()
-    for side in range(2):
-        @pl.when(sends[2][side])
-        def _(side=side):
-            x_copy(side).start()
 
     for side in range(2):
         for dy in (-1, 0, 1):
@@ -146,11 +149,6 @@
     for f in range(fields):
         halo_z[f] = jnp.where(from_left, ends[0, f], ends[1, f])
 
-    for side in range(2):
-        @pl.when(gets[1][side])
-        def _(side=side):
-            y_copy(side).wait_recv()
-
     wide = lax.broadcasted_iota(jnp.int32, (cy, cz), 0)
     far = lax.broadcasted_iota(jnp.int32, (cy, cz), 1)
     uy = ((gy * cy + wide).astype(jnp.float32) + 0.5) / (cy * ngy) - 0.5
@@ -167,6 +165,25 @@
         p2 = pltpu.roll(jnp.where(head, ring, cell), cz - 2, 1)
         return m2, m1, p1, p2
 
+    def z_part(i, _):
+        for u in range(2):
+            x = 2 * i + u
+            for f in range(fields):
+                for half in range(2):
+                    at = pl.ds(8 + 8 * half, 8)
+                    cell = grid[f, x + 2, at, :]
+                    m2, m1, p1, p2 = along(cell, halo_z[f], lax.rem(2 * cz - 2 - 4 * half - 8 * x, cz))
+                    first_z[f, x, at, :] = 8.0 * (p1 - m1) - (p2 - m2)
+                    some[f, x, pl.ds(8 * half, 8), :] = (p2 + m2) - 16.0 * (p1 + m1) - 30.0 * cell
+        return 0
+
+    lax.fori_loop(0, cx // 2, z_part, 0)
+
+    for side in range(2):
+        @pl.when(gets[1][side])
+        def _(side=side):
+            y_copy(side).wait_recv()
+
     for end, (rows, first, slope) in enumerate(((rows_low, 8, slope_low), (rows_high, 0, slope_high))):
         @pl.when(gets[1][end])
         def _(end=end, rows=rows, first=first, slope=slope):
@@ -180,41 +197,29 @@
             slope[...] = jnp.zeros(slope.shape, jnp.float32)
 
 
-    def plane(i, _):
-        x = lax.rem(i + 2, cx)
-
-        @pl.when(i == cx - 4)
-        def _():
-            for side in range(2):
-                @pl.when(gets[2][side])
-                def _(side=side):
-                    x_copy(side).wait_recv()
-
-        shift0 = lax.rem(2 * cz - 2 - 8 * x, cz)
-        shift1 = lax.rem(2 * cz - 6 - 8 * x, cz)
-        combo, mixed = [], []
+    def outer_rows(x, _):
         for f in range(fields):
             base = f * 2 * cx + 2 * x
             outside = jnp.where(row < 4, rows_high[pl.ds(base, 8), :], rows_low[pl.ds(base + 2, 8), :])
+            d = jnp.where(row < 4, slope_high[pl.ds(base, 8), :], slope_low[pl.ds(base + 2, 8), :])
             grid[f, x + 2, pl.ds(0, 8), :] = outside
             grid[f, x + 2, pl.ds(8 + cy, 8), :] = outside
-            d = jnp.where(row < 4, slope_high[pl.ds(base, 8), :], slope_low[pl.ds(base + 2, 8), :])
-            first_z[f, pl.ds(0, 8), :] = d
-            first_z[f, pl.ds(8 + cy, 8), :] = d
-            seconds = []
-            for half in range(2):
-                cell = grid[f, x + 2, pl.ds(8 + 8 * half, 8), :]
-                m2, m1, p1, p2 = along(cell, halo_z[f], shift1 if half else shift0)
-                first_z[f, pl.ds(8 + 8 * half, 8), :] = 8.0 * (p1 - m1) - (p2 - m2)
-                seconds.append(16.0 * (p1 + m1) - (p2 + m2))
-            center = grid[f, x + 2, pl.ds(8, cy), :]
+            first_z[f, x, pl.ds(0, 8), :] = d
+            first_z[f, x, pl.ds(8 + cy, 8), :] = d
+        return 0
+
+    lax.fori_loop(0, cx, outer_rows, 0)
+
+    def stencil(x, u):
+        combo, mixed = [], []
+        for f in range(fields):
             near_xy = (grid[f, x + 1, pl.ds(8, cy), :] + grid[f, x + 3, pl.ds(8, cy), :]
                        + grid[f, x + 2, pl.ds(7, cy), :] + grid[f, x + 2, pl.ds(9, cy), :])
             far_xy = (grid[f, x, pl.ds(8, cy), :] + grid[f, x + 4, pl.ds(8, cy), :]
                       + grid[f, x + 2, pl.ds(6, cy), :] + grid[f, x + 2, pl.ds(10, cy), :])
-            combo.append(16.0 * near_xy - far_xy - 30.0 * center - jnp.concatenate(seconds, 0))
-            mixed.append(8.0 * (first_z[f, pl.ds(9, cy), :] - first_z[f, pl.ds(7, cy), :])
-                         - (first_z[f, pl.ds(10, cy), :] - first_z[f, pl.ds(6, cy), :]))
+            combo.append(16.0 * near_xy - far_xy + some[f, x])
+            mixed.append(8.0 * (first_z[f, x, pl.ds(9, cy), :] - first_z[f, x, pl.ds(7, cy), :])
+                         - (first_z[f, x, pl.ds(10, cy), :] - first_z[f, x, pl.ds(6, cy), :]))
         ux = ((gx * cx + x).astype(jnp.float32) + 0.5) * (1.0 / (cx * ngx)) - 0.5
         rsq = (rsq_yz + ux * ux) * 0.0625
         news_re = jnp.zeros((cy, cz), jnp.float32)
@@ -227,11 +232,10 @@
             news_re, news_im = news_re + re, news_im + im
             flux = rsq * (news_re * news_re + news_im * news_im)
             coarse = flux.astype(jnp.bfloat16).astype(jnp.float32)
-            parts[2 * t] = coarse
-            parts[2 * t + 1] = flux - coarse
-        pltpu.make_async_copy(psi.at[:, x], psi_out.at[:, x], out_sem.at[x]).start()
-
-        total = acc[...]
+            parts[u, 2 * t] = coarse
+            parts[u, 2 * t + 1] = flux - coarse
+
+    def bins(x, u, total):
         group = 4
         for y0 in range(0, cy, group):
             left, right = [], []
@@ -244,16 +248,33 @@
                 right.append(jnp.where(jnp.broadcast_to(low, (n_lo, cz)) == low_label, 1.0, 0.0))
             for p in range(2 * steps):
                 left.append(jnp.concatenate(
-                    [jnp.where(hit[k], jnp.broadcast_to(parts[p, pl.ds(y0 + k, 1), :], (HI, cz)), 0.0)
+                    [jnp.where(hit[k], jnp.broadcast_to(parts[u, p, pl.ds(y0 + k, 1), :], (HI, cz)), 0.0)
                      for k in range(group)], 1))
             total = total + lax.dot_general(
                 jnp.concatenate(left, 0).astype(jnp.bfloat16),
                 jnp.concatenate(right, 1).astype(jnp.bfloat16),
                 (((1,), (1,)), ((), ())), preferred_element_type=jnp.float32)
+        return total
+
+    def pair(i, _):
+        @pl.when(i == cx // 2 - 2)
+        def _():
+            for side in range(2):
+                @pl.when(gets[2][side])
+                def _(side=side):
+                    x_copy(side).wait_recv()
+
+        first = lax.rem(2 * i + 2, cx)
+        for u in range(2):
+            stencil(first + u, u)
+        pltpu.make_async_copy(psi.at[:, pl.ds(first, 2)], psi_out.at[:, pl.ds(first, 2)], out_sem.at[i]).start()
+        total = acc[...]
+        for u in range(2):
+            total = bins(first + u, u, total)
         acc[...] = total
         return 0
 
-    lax.fori_loop(0, cx, plane, 0)
+    lax.fori_loop(0, cx // 2, pair, 0)
 
     for t in range(steps):
         both = acc[pl.ds(16 * t, 8), :] + acc[pl.ds(16 * t + 8, 8), :]
@@ -329,11 +350,12 @@
 
     energy[...] = lax.fori_loop(0, gx, take_line, mine)[:steps, :own]
 
-    def end_out(x, _):
-        pltpu.make_async_copy(psi.at[:, x], psi_out.at[:, x], out_sem.at[x]).wait()
-        return 0
-
-    lax.fori_loop(0, cx, end_out, 0)
+    def end_out(i, _):
+        first = lax.rem(2 * i + 2, cx)
+        pltpu.make_async_copy(psi.at[:, pl.ds(first, 2)], psi_out.at[:, pl.ds(first, 2)], out_sem.at[i]).wait()
+        return 0
+
+    lax.fori_loop(0, cx // 2, end_out, 0)
 
     for side in range(2):
         for dy in (0, -1, 1):
@@ -397,14 +419,15 @@
             pltpu.VMEM((2, fields * 2 * cx, cz), f32),
             pltpu.VMEM((fields * 2 * cx + 8, cz), f32),
             pltpu.VMEM((fields * 2 * cx + 8, cz), f32),
-            pltpu.VMEM((fields, cy + 16, cz), f32),
-            pltpu.VMEM((2 * steps, cy, cz), f32),
+            pltpu.VMEM((fields, cx, cy + 16, cz), f32),
+            pltpu.VMEM((fields, cx, cy, cz), f32),
+            pltpu.VMEM((2, 2 * steps, cy, cz), f32),
             pltpu.VMEM((2 * steps * HI, n_lo), f32),
             pltpu.VMEM((HI, 8, 128), f32),
             pltpu.VMEM((peers, 8, 128), f32),
             pltpu.VMEM((8, 128), f32),
             pltpu.VMEM((ngx, 8, 128), f32),
-            dma((2,)), dma((cx,)),
+            dma((2,)), dma((cx // 2,)),
             dma((2,)), dma((2,)), dma((2,)), dma((2,)), dma((2, 3)), dma((2, 3)),
             dma((peers,)), dma((peers,)), dma((ngx,)), dma((ngx,)),
         ],

time: 27.8 us -> 28.2 us (1.014)
  Pallas kernels: 24.1 us -> 24.5 us
    pallas_call x1, Pallas kernels: 24.1 us -> 24.5 us  [body(): pl.pallas_call(functools.partial(step, sizes), out_shape=(jax.ShapeDtypeS...]
where the time goes in v3:
time: 28.2 us; the launch traced here: 28 us
  Pallas kernels  24.5 us (87%)
  local copies, waits for them, and re-layouts  2.85 us (10%)
  between operations  0.65 us (2%)
    pallas_call x1, Pallas kernels, body(): pl.pallas_call(functools.partial(step, sizes), out_shape=(jax.ShapeDtypeS...  24.5 us
    unnamed x4, local copies, waits for them, and re-layouts  2.85 us

profile of v3, /device:TPU:0, one launch (start us, length us, event | category | flops | bytes accessed | tf_op | source)
XLA Modules:
  0.0 28.0 jit_solution(16642131443042718508)
XLA Ops:
  0.6 24.5 %shard_map.50 = (f32[8,16,16,128]{3,2,1,0:T(8,128)}, f32[4,32]{1,0:T(4,128)}) custom-call(f32[8,16,16,128]{3,2,1,0:T(8,128)} %bitcast.4, s32[16,16,128]{2,1,0:T(8,128)} %cells.1, s32[1,256]{1,0:T(1,128)} %bitcast.7), custom_call_target="tpu_custom_call" | custom-call | tf_op jit(solution)/shard_map/pallas_call | solution.py:400
  25.1 0.0 copy-start
  25.2 2.3 %copy.7 = f32[2,4,16,16,128]{4,3,2,1,0:T(8,128)} copy(f32[2,4,16,16,128]{4,3,2,1,0:T(8,128)} %bitcast.5) | data formatting | bytes 2097152
  27.4 0.0 copy-done
  27.4 0.6 %copy.8 = f32[1,4,32]{2,1,0:T(4,128)} copy(f32[1,4,32]{2,1,0:T(4,128)S(1)} %bitcast.6) | data formatting | bytes 1024
Async XLA Ops:
  25.1 2.3 %copy-start = (f32[4,32]{1,0:T(4,128)S(1)}, f32[4,32]{1,0:T(4,128)}, u32[]{:S(2)}) copy-start(f32[4,32]{1,0:T(4,128)} %get-tuple-element.5) | copy-start | bytes 1540
